TPU v7x, 1024 devices: a whole 4x8x16 slice. The times are simulated.
1024 devices in a mesh: node: 64 (over y, x, core), chip: 16 (over z).
Axes of the slice: x: 4, y: 8, z: 16, core: 2. Of those that a mesh axis runs over, the one named last changes fastest.
Arguments:
- momentum: float32 [1024, 128, 512], P(('node', 'chip')), may hold values from -6 to 6
- gradient: bfloat16 [1024, 128, 512], P(('node', 'chip')), may hold values from -6 to 6
- indices: int32 [1024, 16, 32], P(('node', 'chip')), may hold values from 0 to 4095, as said below
Outputs:
- new_momentum: float32 [1024, 128, 512], P(('node', 'chip'))
- update: float32 [128, 512], replicated
Inputs may be any that keep to these rules, and one draw needn't show every extreme that they name: `indices`: the 32 entries of each row name distinct coefficients of their span, coefficient (k, l) being k * 64 + l.
All inputs are finite; a program needn't handle non-finite values.
Results may differ from a plain program's by a relative error of at most 0.0029.
Values may be sent and summed in bfloat16 or wider, within the bound.
A program may use at most 64 MiB of HBM per device.

v0:
```python
import functools
import math

import jax
import jax.numpy as jnp
from jax import lax
from jax.sharding import Mesh
from jax.sharding import PartitionSpec as P

SPAN = 64
NODE = ("node_0", "node_1", "node_2")
NODE_CHIP = ("node_0", "node_1", "node_2", "chip")


def from_everyone(array, axis):
    devices = lax.axis_size(axis)
    return lax.all_to_all(
        jnp.broadcast_to(array[None], (devices, *array.shape)), axis, 0, 0, tiled=True
    )


def laid_out(parts, dim):
    parts = jnp.moveaxis(parts, 0, dim)
    shape = parts.shape
    return parts.reshape(*shape[:dim], shape[dim] * shape[dim + 1], *shape[dim + 2 :])


def gathered_copies(array, axis, dim):
    parts = from_everyone(array, axis)
    return laid_out(parts, dim)


def by_axis(array, axes):
    return functools.reduce(lax.psum, axes, array)


def dct_table(edge_len):
    orders = jnp.arange(edge_len, dtype=jnp.float32)
    wave_no = orders[:, None]
    cell_no = orders[None, :]
    factor = jnp.where(wave_no == 0.0, math.sqrt(1.0 / edge_len), math.sqrt(2.0 / edge_len))
    return factor * jnp.cos(math.pi * (2.0 * cell_no + 1.0) * wave_no / (2.0 * edge_len))


def forward(grid_field, cosines, edge_len):
    row_blocks = grid_field.shape[0] // edge_len
    col_blocks = grid_field.shape[1] // edge_len
    blocks = grid_field.reshape(row_blocks, edge_len, col_blocks, edge_len).transpose(0, 2, 1, 3)
    coeffs = jnp.einsum(
        "kn,abnm,lm->abkl", cosines, blocks, cosines, precision=lax.Precision.HIGHEST
    )
    return coeffs.reshape(row_blocks * col_blocks, edge_len * edge_len)


def inverse_blocks(coeffs, cosines, edge_len):
    blocks = coeffs.reshape(coeffs.shape[0], edge_len, edge_len)
    return jnp.einsum("kn,ckl,lm->cnm", cosines, blocks, cosines, precision=lax.Precision.HIGHEST)


def place_blocks(blocks, row_count, col_count, edge_len):
    shaped = blocks.reshape(row_count // edge_len, col_count // edge_len, edge_len, edge_len)
    return shaped.transpose(0, 2, 1, 3).reshape(row_count, col_count)


def normalized(blocks):
    energy = jnp.mean(blocks * blocks, axis=(1, 2), keepdims=True)
    return blocks / jnp.sqrt(energy + 1.0)


def decode_block(picked, slots):
    n_spans = picked.shape[1]
    values_rows = jnp.moveaxis(picked, 1, 0).reshape(n_spans, -1)
    slot_rows = jnp.moveaxis(slots, 1, 0).reshape(n_spans, -1)
    orders = jnp.arange(SPAN, dtype=jnp.int32)[None, :]

    def one_span(pair):
        vals, where = pair
        wave_rows = (where // SPAN)[:, None] == orders
        wave_cols = (where % SPAN)[:, None] == orders
        left_hot = wave_rows.astype(jnp.bfloat16)
        right_hot = jnp.where(wave_cols, vals[:, None], jnp.zeros((), jnp.bfloat16))
        block = lax.dot_general(
            left_hot, right_hot, (((0,), (0,)), ((), ())), preferred_element_type=jnp.float32
        )
        return block.reshape(SPAN * SPAN)

    return lax.map(one_span, (values_rows, slot_rows))


def decode_lists(totals, picked, slots):
    count = picked.shape[0]
    group_len = 1
    for trial in range(1, 17):
        if count % trial == 0:
            group_len = trial
    picked_groups = picked.reshape((count // group_len, group_len) + picked.shape[1:])
    slot_groups = slots.reshape((count // group_len, group_len) + slots.shape[1:])

    def add_group(step, carry):
        return carry + decode_block(picked_groups[step], slot_groups[step])

    return lax.fori_loop(0, count // group_len, add_group, totals)


def shards(momentum, gradient, indices):
    cosines = dct_table(SPAN)
    row_count = momentum.shape[1]
    col_count = momentum.shape[2]
    blended = 0.9 * momentum[0] + gradient[0].astype(jnp.float32)
    coeffs = forward(blended, cosines, SPAN)
    slots = indices[0]
    picked = jnp.take_along_axis(coeffs, slots, axis=1).astype(jnp.bfloat16)
    sparse = decode_block(picked[None], indices)
    own_part = place_blocks(inverse_blocks(sparse, cosines, SPAN), row_count, col_count, SPAN)
    new_momentum = (blended - own_part)[None]
    partial_sum = decode_lists(
        jnp.zeros_like(coeffs),
        gathered_copies(picked[None], "chip", 0),
        gathered_copies(indices, "chip", 0),
    )
    totals = by_axis(partial_sum, NODE)
    update = place_blocks(
        normalized(inverse_blocks(totals, cosines, SPAN)), row_count, col_count, SPAN
    )
    return (new_momentum, update)


def solution(mesh):
    finer = Mesh(
        mesh.devices.reshape(8, 4, 2, mesh.shape["chip"]), ("node_0", "node_1", "node_2", "chip")
    )
    placed = (P(NODE_CHIP, None, None), P(NODE_CHIP, None, None), P(NODE_CHIP, None, None))
    return jax.shard_map(
        shards,
        mesh=finer,
        in_specs=placed,
        out_specs=(P(NODE_CHIP, None, None), P()),
        check_vma=False,
    )
```

profile of v0, /device:TPU:1, one launch (start us, length us, event | category | flops | bytes accessed | tf_op | source)
XLA Modules:
  0.0 294.6 jit_solution(3653685282893450361)
XLA Ops:
  7.2 1.1 convert_add_fusion
  8.6 1.7 fusion.21
  10.3 0.7 fusion.23
  11.3 0.4 copy-done.1
  11.8 4.8 %gather_fusion = bf16[512]{0:T(512)(128)(2,1)S(1)} fusion(bf16[16,4096]{1,0:T(8,128)(2,1)S(1)} %reshape.236, s32[512]{0:T(512)S(1)} %reshape.245), kind=kCustom, calls=%fused_computation | custom fusion | bytes 6144 | tf_op jit(solution)/shard_map/jit(take_along_axis)/gather | solution.py:112
  16.7 0.7 reshape.256
  17.5 19.4 %all-to-all-start.1 = ((bf16[16,2,256]{2,1,0:T(2,128)(2,1)}), bf16[16,2,256]{2,1,0:T(2,128)(2,1)S(1)}, u32[]{:S(2)}, u32[]{:S(2)}) async-start(bf16[16,2,256]{2,1,0:T(2,128)(2,1)} %reshape.256), calls=%async_computation.1 | async-start | bytes 32768 | tf_op jit(solution)/shard_map/all_to_all | solution.py:17
  36.9 0.7 reshape.254
  37.6 10.6 %all-to-all-done.1 = bf16[16,2,256]{2,1,0:T(2,128)(2,1)S(1)} async-done(((bf16[16,2,256]{2,1,0:T(2,128)(2,1)}), bf16[16,2,256]{2,1,0:T(2,128)(2,1)S(1)}, u32[]{:S(2)}, u32[]{:S(2)}) %all-to-all-start.1) | async-done | bytes 16416 | tf_op jit(solution)/shard_map/all_to_all | solution.py:17
  48.3 3.5 %all-to-all-start = ((s32[16,1,512]{2,1,0:T(1,128)}), s32[16,1,512]{2,1,0:T(1,128)S(1)}, u32[]{:S(2)}, u32[]{:S(2)}) async-start(s32[16,1,512]{2,1,0:T(1,128)} %reshape.254), calls=%async_computation | async-start | bytes 65536 | tf_op jit(solution)/shard_map/all_to_all | solution.py:17
  52.1 11.1 %all-to-all-done = s32[16,1,512]{2,1,0:T(1,128)S(1)} async-done(((s32[16,1,512]{2,1,0:T(1,128)}), s32[16,1,512]{2,1,0:T(1,128)S(1)}, u32[]{:S(2)}, u32[]{:S(2)}) %all-to-all-start) | async-done | bytes 32800 | tf_op jit(solution)/shard_map/all_to_all | solution.py:17
  63.1 0.5 broadcast.327
  63.6 0.7 reduce.2
  64.6 17.1 %while.37 = (s32[]{:T(128)}, f32[16,4096]{1,0:T(8,128)S(1)}, s32[16,512]{1,0:T(8,128)S(1)}, bf16[16,512]{1,0:T(8,128)(2,1)S(1)}, s32[]{:T(128)}, /*index=5*/s32[]{:T(128)}) while((s32[]{:T(128)}, f32[16,4096]{1,0:T(8,128)S(1)}, s32[16,512]{1,0:T(8,128)S(1)}, bf16[16,512]{1,0:T(8,128)(2,1)S(1)}, s32[]{:T(128)}, ...), condition=%wide.region_3.4_spmd.clone.clone, body=%wide.region_2.3_spmd.clone.clone.sunk | while | flops 4302338 | bytes 99409 | solution.py:87
  64.7 0.5 fusion.73
  65.8 0.5 fusion.73
  66.9 0.5 fusion.73
  67.4 0.4 dynamic_update_slice.20
  67.9 0.5 fusion.73
  68.5 0.4 dynamic_update_slice.20
  69.0 0.5 fusion.73
  70.1 0.5 fusion.73
  71.1 0.5 fusion.73
  71.7 0.4 dynamic_update_slice.20
  72.2 0.5 fusion.73
  72.8 0.4 dynamic_update_slice.20
  73.3 0.5 fusion.73
  73.8 0.4 dynamic_update_slice.20
  74.3 0.5 fusion.73
  75.4 0.5 fusion.73
  76.5 0.5 fusion.73
  77.5 0.5 fusion.73
  78.6 0.5 fusion.73
  79.7 0.5 fusion.73
  80.7 0.5 fusion.73
  81.7 0.7 copy-done
  82.5 78.3 %all-reduce.4.cloned.1.call-done = f32[16,4096]{1,0:T(8,128)} async-done(((f32[16,4096]{1,0:T(8,128)}), f32[16,4096]{1,0:T(8,128)}) %all-reduce.4.cloned.1.call-update) | async-done | bytes 262160 | tf_op jit(solution)/shard_map/psum | solution.py:34
  160.9 13.3 %while.36 = (s32[]{:T(128)}, f32[16,4096]{1,0:T(8,128)S(1)}, s32[16,32]{1,0:T(8,128)S(1)}, bf16[16,32]{1,0:T(8,128)(2,1)S(1)}, s32[]{:T(128)}, /*index=5*/s32[]{:T(128)}) while((s32[]{:T(128)}, f32[16,4096]{1,0:T(8,128)S(1)}, s32[16,32]{1,0:T(8,128)S(1)}, bf16[16,32]{1,0:T(8,128)(2,1)S(1)}, s32[]{:T(128)}, ...), condition=%wide.region_1.2_spmd.clone.clone, body=%wide.region_0.1_spmd.clone.clone.sunk | while | flops 268930 | bytes 83089 | solution.py:87
  174.4 53.9 %all-reduce.6.cloned.1.call-done = f32[16,4096]{1,0:T(8,128)} async-done(((f32[16,4096]{1,0:T(8,128)}), f32[16,4096]{1,0:T(8,128)}) %all-reduce.6.cloned.1.call-update) | async-done | bytes 262160 | tf_op jit(solution)/shard_map/psum | solution.py:34
  228.4 1.1 reshape.242
  229.5 1.0 copy.23
  230.5 0.7 fusion.32
  231.3 0.7 fusion.30
  232.4 0.7 sub.16
  233.2 50.1 %all-reduce.8.cloned.1.call-done = f32[16,64,64]{1,2,0:T(8,128)} async-done(((f32[16,64,64]{1,2,0:T(8,128)}), f32[16,64,64]{1,2,0:T(8,128)}) %all-reduce.8.cloned.1.call-update) | async-done | bytes 262160 | tf_op jit(solution)/shard_map/psum | solution.py:34
  283.2 2.8 fusion.28
  286.0 0.8 multiply_reduce_fusion
  287.3 0.9 reshape.244
  (203 shorter events, 21.6 us)
Async XLA Ops:
  11.0 0.7 copy-start.1
  17.5 30.8 %all-to-all-start.1 = ((bf16[16,2,256]{2,1,0:T(2,128)(2,1)}), bf16[16,2,256]{2,1,0:T(2,128)(2,1)S(1)}, u32[]{:S(2)}, u32[]{:S(2)}) async-start(bf16[16,2,256]{2,1,0:T(2,128)(2,1)} %reshape.256), calls=%async_computation.1 | async-start | bytes 32768 | tf_op jit(solution)/shard_map/all_to_all | solution.py:17
  48.3 14.9 %all-to-all-start = ((s32[16,1,512]{2,1,0:T(1,128)}), s32[16,1,512]{2,1,0:T(1,128)S(1)}, u32[]{:S(2)}, u32[]{:S(2)}) async-start(s32[16,1,512]{2,1,0:T(1,128)} %reshape.254), calls=%async_computation | async-start | bytes 65536 | tf_op jit(solution)/shard_map/all_to_all | solution.py:17
  51.8 109.0 %all-reduce.4.cloned.1.call-start = ((), (), s32[]{:S(2)}) async-start(), calls=%async_computation.2 | async-start | bytes 524288 | tf_op jit(solution)/shard_map/psum | solution.py:34
  81.7 0.7 copy-start
  82.4 145.9 %all-reduce.6.cloned.1.call-start = ((), (), s32[]{:S(2)}) async-start(), calls=%async_computation.3 | async-start | bytes 524288 | tf_op jit(solution)/shard_map/psum | solution.py:34
  160.8 122.4 %all-reduce.8.cloned.1.call-start = ((), (), s32[]{:S(2)}) async-start(), calls=%async_computation.4 | async-start | bytes 1048576 | tf_op jit(solution)/shard_map/psum | solution.py:34
Sparse Core Ops, SparseCore 0:
  82.6 78.1 all-reduce.3
  163.1 65.2 all-reduce.5
  231.8 51.3 all-reduce.7
where the time goes:
time: 295 us
  waiting for transfers between devices  204 us (69%)
  local copies, waits for them, and re-layouts  29.5 us (10%)
  starting transfers between devices  23 us (8%)
  matrix products  19.4 us (7%)
  between operations  14 us (5%)
  other arithmetic  3.19 us (1%)
    psum x3, waiting for transfers between devices, by_axis(): return functools.reduce(lax.psum, axes, array)  182 us
    all_to_all x2, starting transfers between devices, from_everyone(): lax.all_to_all(jnp.broadcast_to(array[None], (devices, *array.shape)), ax...  22.9 us
    all_to_all x2, waiting for transfers between devices, from_everyone(): lax.all_to_all(jnp.broadcast_to(array[None], (devices, *array.shape)), ax...  21.7 us
    dynamic_update_slice x32, local copies, waits for them, and re-layouts, decode_block(): return lax.map(one_span, (values_rows, slot_rows))  12.6 us
    dot_general x32, matrix products, one_span(): lax.dot_general(left_hot, right_hot, (((0,), (0,)), ((), ())), preferred_...  12 us
  transfers between devices with their start and end apart: 5, of which 5 were waited for; matrix products, arithmetic and copies ran while one was open for 6% of the time, Pallas kernels for 0%

commit v1 on v0

v1 whole, which is shorter than its diff:
```python
import functools

import jax
import jax.numpy as jnp
import ml_dtypes
import numpy as np
from jax import lax
from jax.experimental import pallas as pl
from jax.experimental.pallas import tpu as pltpu
from jax.sharding import PartitionSpec as P

MESH = pl.DeviceIdType.MESH
SPAN = 64
GROUP = 8
F32 = jnp.float32
BF16 = jnp.bfloat16


def cosine_tables():
    orders = np.arange(SPAN, dtype=np.float64)
    scale = np.where(orders == 0, np.sqrt(1.0 / SPAN), np.sqrt(2.0 / SPAN))[:, None]
    table = scale * np.cos(np.pi * (2 * orders[None, :] + 1) * orders[:, None] / (2 * SPAN))
    high = table.astype(ml_dtypes.bfloat16)
    low = (table - high.astype(np.float64)).astype(ml_dtypes.bfloat16)
    zero = np.zeros_like(high)
    picker = np.concatenate([high.T, low.T], axis=0)
    right = np.concatenate(
        [np.block([[part, zero], [zero, part]]) for part in (high, low)], axis=0
    )
    left = np.concatenate([high.T, high.T, low.T], axis=1)
    return picker, right, left


def split(x):
    high = x.astype(BF16)
    low = (x - high.astype(F32)).astype(BF16)
    return high, low


def mm(a, b):
    return jnp.dot(a, b, preferred_element_type=F32)


def mm_nt(a, b):
    return lax.dot_general(a, b, (((1,), (1,)), ((), ())), preferred_element_type=F32)


def far_first(n):
    return sorted(range(1, n), key=lambda d: -min(d, n - d))


def kernel(
    ys, zs, mom, grad, idx, picker_h, right_h, left_h,
    newm, upd,
    mbuf, gbuf, ibuf, picker, right, left, nbuf,
    msg, lists, zbuf, ybuf, ubuf,
    in_sem, out_sem, s1, r1, s2, r2, s3, r3, s4, r4,
):
    node = lax.axis_index("node")
    z = lax.axis_index("chip")
    p = lax.rem(node, GROUP)
    y = lax.div(node, GROUP)

    loads = [
        pltpu.make_async_copy(src, dst, in_sem.at[i])
        for i, (src, dst) in enumerate(
            [(idx.at[0], ibuf), (picker_h, picker), (mom.at[0], mbuf), (grad.at[0], gbuf),
             (right_h, right), (left_h, left)]
        )
    ]
    for load in loads:
        load.start()

    def group_peer(d):
        return (y * GROUP + lax.rem(p + d, GROUP), z)

    def y_peer(d):
        return (lax.rem(y + d, ys) * GROUP + p, z)

    def z_peer(d):
        return (node, lax.rem(z + d, zs))

    barrier = pltpu.get_barrier_semaphore()
    peers = (
        [z_peer(d) for d in far_first(zs)]
        + [y_peer(d) for d in far_first(ys)]
        + [group_peer(d) for d in far_first(GROUP)]
    )
    for peer in peers:
        pl.semaphore_signal(barrier, inc=1, device_id=peer, device_id_type=MESH)

    lane4 = lax.broadcasted_iota(jnp.int32, (4, 128), 1)
    lane64 = lax.broadcasted_iota(jnp.int32, (SPAN, 128), 1)
    row64 = lax.broadcasted_iota(jnp.int32, (SPAN, 128), 0)
    row128 = lax.broadcasted_iota(jnp.int32, (128, 128), 0)

    loads[0].wait()
    slots = jnp.concatenate([ibuf[pl.ds(j, 4, stride=4), :] for j in range(4)], axis=1)
    wave_k = slots >> 6
    wave_l = slots & 63
    hot = [(row64 == wave_k[q : q + 1]).astype(F32).astype(BF16) for q in range(4)]
    hot += [(row64 == wave_l[q : q + 1]).astype(F32).astype(BF16) for q in range(4)]
    loads[1].wait()
    waves = mm(picker[...], jnp.concatenate(hot, axis=1))
    span_of = lane64 // 32

    def spread(part):
        return jnp.concatenate(
            [jnp.where(span_of == j, part, 0.0) for j in range(4)], axis=0
        ).astype(BF16)

    cols_high = [spread(waves[0:64, 512 + 128 * q : 640 + 128 * q]) for q in range(4)]
    cols_low = [spread(waves[64:128, 512 + 128 * q : 640 + 128 * q]) for q in range(4)]
    rows_all = [
        waves[0:64, 128 * q : 128 * q + 128] + waves[64:128, 128 * q : 128 * q + 128]
        for q in range(4)
    ]

    loads[2].wait()
    loads[3].wait()
    picked = []
    for q in range(4):
        rows = slice((q // 2) * 64, (q // 2) * 64 + 64)
        cols = slice((q % 2) * 256, (q % 2) * 256 + 256)
        blended = 0.9 * mbuf[rows, cols] + gbuf[rows, cols].astype(F32)
        mbuf[rows, cols] = blended
        high, low = split(blended)
        half = mm(high, cols_high[q]) + mm(low, cols_high[q]) + mm(high, cols_low[q])
        picked.append(jnp.sum(half * rows_all[q], axis=0, keepdims=True).astype(BF16).astype(F32))

    values = jnp.concatenate(picked, axis=0)
    where = slots.astype(F32)
    even = jnp.where(lane4 < 64, values, pltpu.roll(where, 64, 1))
    odd = jnp.where(lane4 < 64, pltpu.roll(values, 64, 1), where)
    for q in range(4):
        msg[2 * q] = even[q : q + 1]
        msg[2 * q + 1] = odd[q : q + 1]
    lists[p] = msg[p]

    pl.semaphore_wait(barrier, len(peers))

    first = []
    for d in far_first(GROUP):
        peer = group_peer(d)
        copy = pltpu.make_async_remote_copy(
            src_ref=msg.at[lax.rem(p + d, GROUP)], dst_ref=lists.at[p],
            send_sem=s1.at[d - 1], recv_sem=r1.at[d - 1],
            device_id=peer, device_id_type=MESH,
        )
        copy.start()
        first.append(copy)

    stores = []
    for q in range(4):
        rows = slice((q // 2) * 64, (q // 2) * 64 + 64)
        cols = slice((q % 2) * 256, (q % 2) * 256 + 256)
        high, low = split(rows_all[q] * picked[q])
        own = mm_nt(high, cols_high[q]) + mm_nt(low, cols_high[q]) + mm_nt(high, cols_low[q])
        nbuf[rows, cols] = mbuf[rows, cols] - own
    store = pltpu.make_async_copy(nbuf, newm.at[0], out_sem.at[0])
    store.start()

    for copy in first:
        copy.wait_recv()

    got = lists[...].reshape(GROUP, 128)
    top, bottom = got[0:4], got[4:8]
    zbuf[z] = jnp.concatenate(
        [
            jnp.where(lane4 < 64, top, pltpu.roll(bottom, 64, 1)),
            jnp.where(lane4 < 64, pltpu.roll(top, 64, 1), bottom),
        ],
        axis=0,
    )
    second = []
    for d in far_first(zs):
        copy = pltpu.make_async_remote_copy(
            src_ref=zbuf.at[z], dst_ref=zbuf.at[z],
            send_sem=s2.at[d - 1], recv_sem=r2.at[d - 1],
            device_id=z_peer(d), device_id_type=MESH,
        )
        copy.start()
        second.append(copy)
    loads[4].wait()
    loads[5].wait()
    for copy in second:
        copy.wait_recv()

    def decode(step, total):
        tile = zbuf[step]
        vals = tile[0:4]
        spot = tile[4:8].astype(jnp.int32)
        at_k = spot >> 6
        at_l = (spot & 63) + ((lane4 // 32) % 2) * 64
        hot_rows, hot_cols = [], []
        for c in range(4):
            hot_rows.append((row64 == at_k[c : c + 1]).astype(F32).astype(BF16))
            hot_cols.append(jnp.where(row128 == at_l[c : c + 1], vals[c : c + 1], 0.0).astype(BF16))
        return total + mm_nt(
            jnp.concatenate(hot_rows, axis=1), jnp.concatenate(hot_cols, axis=1)
        )

    total = lax.fori_loop(0, zs, decode, jnp.zeros((SPAN, 128), F32))

    ybuf[y] = total.astype(BF16)
    third = []
    for d in far_first(ys):
        copy = pltpu.make_async_remote_copy(
            src_ref=ybuf.at[y], dst_ref=ybuf.at[y],
            send_sem=s3.at[d - 1], recv_sem=r3.at[d - 1],
            device_id=y_peer(d), device_id_type=MESH,
        )
        copy.start()
        third.append(copy)
    for copy in third:
        copy.wait_recv()
    total = ybuf[0].astype(F32)
    for i in range(1, ys):
        total = total + ybuf[i].astype(F32)

    high, low = split(total)
    half = mm(high, right[0:128]) + mm(low, right[0:128]) + mm(high, right[128:256])
    high, low = split(half)
    field = mm(left[...], jnp.concatenate([high, low, high], axis=0))
    energy = jnp.sum(total * total, axis=0, keepdims=True)
    lane1 = lax.broadcasted_iota(jnp.int32, (1, 128), 1)
    one = jnp.sum(jnp.where(lane1 < 64, energy, 0.0), axis=1, keepdims=True)
    two = jnp.sum(jnp.where(lane1 < 64, 0.0, energy), axis=1, keepdims=True)
    mean = jnp.where(lane1 < 64, one, two) * (1.0 / (SPAN * SPAN))
    ubuf[p] = (field / jnp.sqrt(mean + 1.0)).astype(BF16)

    fourth = []
    for d in far_first(GROUP):
        copy = pltpu.make_async_remote_copy(
            src_ref=ubuf.at[p], dst_ref=ubuf.at[p],
            send_sem=s4.at[d - 1], recv_sem=r4.at[d - 1],
            device_id=group_peer(d), device_id_type=MESH,
        )
        copy.start()
        fourth.append(copy)
    for copy in first + second + third:
        copy.wait_send()
    store.wait()
    for copy in fourth:
        copy.wait_recv()
    for i in range(GROUP):
        upd[(i // 4) * 64 : (i // 4) * 64 + 64, (i % 4) * 128 : (i % 4) * 128 + 128] = ubuf[
            i
        ].astype(F32)
    for copy in fourth:
        copy.wait_send()


def solution(mesh):
    zs = mesh.shape["chip"]
    ys = mesh.shape["node"] // GROUP
    tables = cosine_tables()

    def step(momentum, gradient, indices):
        anywhere = pl.BlockSpec(memory_space=pl.ANY)
        dma = pltpu.SemaphoreType.DMA
        return pl.pallas_call(
            functools.partial(kernel, ys, zs),
            out_shape=(
                jax.ShapeDtypeStruct(momentum.shape, F32),
                jax.ShapeDtypeStruct(momentum.shape[1:], F32),
            ),
            in_specs=[anywhere] * 6,
            out_specs=(anywhere, pl.BlockSpec(memory_space=pltpu.VMEM)),
            scratch_shapes=[
                pltpu.VMEM((128, 512), F32),
                pltpu.VMEM((128, 512), BF16),
                pltpu.VMEM((16, 32), jnp.int32),
                pltpu.VMEM((128, 64), BF16),
                pltpu.VMEM((256, 128), BF16),
                pltpu.VMEM((64, 192), BF16),
                pltpu.VMEM((128, 512), F32),
                pltpu.VMEM((GROUP, 1, 128), F32),
                pltpu.VMEM((GROUP, 1, 128), F32),
                pltpu.VMEM((zs, 8, 128), F32),
                pltpu.VMEM((ys, SPAN, 128), BF16),
                pltpu.VMEM((GROUP, SPAN, 128), BF16),
                dma((6,)),
                dma((1,)),
                dma((GROUP - 1,)),
                dma((GROUP - 1,)),
                dma((max(zs - 1, 1),)),
                dma((max(zs - 1, 1),)),
                dma((max(ys - 1, 1),)),
                dma((max(ys - 1, 1),)),
                dma((GROUP - 1,)),
                dma((GROUP - 1,)),
            ],
            compiler_params=pltpu.CompilerParams(collective_id=0, has_side_effects=True),
        )(momentum, gradient, indices, *(jnp.asarray(t) for t in tables))

    rows = P(("node", "chip"), None, None)
    return jax.shard_map(
        step, mesh=mesh, in_specs=(rows, rows, rows), out_specs=(rows, P()), check_vma=False
    )
```

time: 295 us -> 52.4 us (0.18)
  waiting for transfers between devices: 204 us -> 0 us
  Pallas kernels: 0 us -> 49.2 us
  local copies, waits for them, and re-layouts: 29.5 us -> 2.42 us
  starting transfers between devices: 23 us -> 0 us
  matrix products: 19.4 us -> 0 us
  between operations: 14 us -> 0.65 us
  other arithmetic: 3.19 us -> 0 us
    psum x3 -> x0, waiting for transfers between devices: 182 us -> none  [by_axis(): return functools.reduce(lax.psum, axes, array)]
    pallas_call x0 -> x1, Pallas kernels: none -> 49.2 us  [step(): pl.pallas_call(functools.partial(kernel, ys, zs), out_shape=(jax.ShapeDty...]
    all_to_all x2 -> x0, starting transfers between devices: 22.9 us -> none  [from_everyone(): lax.all_to_all(jnp.broadcast_to(array[None], (devices, *array.shape)), ax...]
    all_to_all x2 -> x0, waiting for transfers between devices: 21.7 us -> none  [from_everyone(): lax.all_to_all(jnp.broadcast_to(array[None], (devices, *array.shape)), ax...]
    dot_general x38 -> x0, matrix products: 19.4 us -> none  [the longest x32 12 us: one_span(): lax.dot_general(left_hot, right_hot, (((0,), (0,)), ((), ())), preferred_...]
    dynamic_update_slice x32 -> x0, local copies, waits for them, and re-layouts: 12.6 us -> none  [decode_block(): return lax.map(one_span, (values_rows, slot_rows))]
    gather x3 -> x0, local copies, waits for them, and re-layouts: 5 us -> none  [shards(): picked = jnp.take_along_axis(coeffs, slots, axis=1).astype(jnp.bfloat16)]
    reshape x8 -> x0, local copies, waits for them, and re-layouts: 3.84 us -> none  [the longest x3 2.34 us: inverse_blocks(): blocks = coeffs.reshape(coeffs.shape[0], edge_len, edge_len)]
  transfers between devices with their start and end apart: 5 -> 0, of which waited for: 5 -> 0; matrix products, arithmetic and copies ran while one was open for 6% -> 0% of each run, Pallas kernels for 0% -> 0%
where the time goes in v1:
time: 52.4 us; the launch traced here: 52.3 us
  Pallas kernels  49.2 us (94%)
  local copies, waits for them, and re-layouts  2.42 us (5%)
  between operations  0.65 us (1%)
    pallas_call x1, Pallas kernels, step(): pl.pallas_call(functools.partial(kernel, ys, zs), out_shape=(jax.ShapeDty...  49.2 us
    unnamed x4, local copies, waits for them, and re-layouts  2.42 us

profile of v1, /device:TPU:1, one launch (start us, length us, event | category | flops | bytes accessed | tf_op | source)
XLA Modules:
  0.0 52.3 jit_solution(12751432344871251530)
XLA Ops:
  0.6 49.2 %shard_map.77 = (f32[1,128,512]{2,1,0:T(8,128)}, f32[128,512]{1,0:T(8,128)}) custom-call(f32[1,128,512]{2,1,0:T(8,128)} %mom.1, bf16[1,128,512]{2,1,0:T(8,128)(2,1)} %grad.1, s32[1,16,32]{2,1,0:T(8,128)} %idx.1, bf16[128,64]{1,0:T(8,128)(2,1)} %constant.6.clone.picker_h, bf16[256,128]{1,0:T(8,128)(2,1)} %constant.7.clone.right_h, ...), custom_call_target="tpu_custom_call" | custom-call | tf_op jit(solution)/shard_map/pallas_call | solution.py:262
  49.8 0.0 copy-start
  49.8 1.7 %copy.10 = f32[1,128,512]{2,1,0:T(8,128)} copy(f32[1,128,512]{2,1,0:T(8,128)} %get-tuple-element.4) | data formatting | bytes 524288
  51.6 0.0 copy-done
  51.6 0.7 %copy.11 = f32[128,512]{1,0:T(8,128)} copy(f32[128,512]{1,0:T(8,128)S(1)} %copy-done) | data formatting | bytes 524288
Async XLA Ops:
  49.8 1.7 %copy-start = (f32[128,512]{1,0:T(8,128)S(1)}, f32[128,512]{1,0:T(8,128)}, u32[]{:S(2)}) copy-start(f32[128,512]{1,0:T(8,128)} %get-tuple-element.5) | copy-start | bytes 786436

commit v2 on v1

--- a/solution.py
+++ b/solution.py
@@ -53,8 +53,8 @@
     ys, zs, mom, grad, idx, picker_h, right_h, left_h,
     newm, upd,
     mbuf, gbuf, ibuf, picker, right, left, nbuf,
-    msg, lists, zbuf, ybuf, ubuf,
-    in_sem, out_sem, s1, r1, s2, r2, s3, r3, s4, r4,
+    msg, zbuf, ybuf, ubuf,
+    in_sem, out_sem, s1, r1, s3, r3, s4, r4,
 ):
     node = lax.axis_index("node")
     z = lax.axis_index("chip")
@@ -77,15 +77,13 @@
     def y_peer(d):
         return (lax.rem(y + d, ys) * GROUP + p, z)
 
-    def z_peer(d):
-        return (node, lax.rem(z + d, zs))
-
     barrier = pltpu.get_barrier_semaphore()
-    peers = (
-        [z_peer(d) for d in far_first(zs)]
-        + [y_peer(d) for d in far_first(ys)]
-        + [group_peer(d) for d in far_first(GROUP)]
-    )
+    peers = [
+        (y * GROUP + lax.rem(p + d, GROUP), lax.rem(z + dz, zs))
+        for dz in far_first(zs)
+        for d in range(GROUP)
+    ]
+    peers += [y_peer(d) for d in far_first(ys)] + [group_peer(d) for d in far_first(GROUP)]
     for peer in peers:
         pl.semaphore_signal(barrier, inc=1, device_id=peer, device_id_type=MESH)
 
@@ -135,20 +133,19 @@
     for q in range(4):
         msg[2 * q] = even[q : q + 1]
         msg[2 * q + 1] = odd[q : q + 1]
-    lists[p] = msg[p]
 
     pl.semaphore_wait(barrier, len(peers))
 
-    first = []
-    for d in far_first(GROUP):
-        peer = group_peer(d)
-        copy = pltpu.make_async_remote_copy(
-            src_ref=msg.at[lax.rem(p + d, GROUP)], dst_ref=lists.at[p],
-            send_sem=s1.at[d - 1], recv_sem=r1.at[d - 1],
-            device_id=peer, device_id_type=MESH,
-        )
-        copy.start()
-        first.append(copy)
+    own_list = pltpu.make_async_copy(msg.at[p], zbuf.at[z * GROUP + p], r1.at[z])
+    own_list.start()
+    rows_sent = [lax.rem(p + d, GROUP) for d in range(GROUP)]
+    for dz in far_first(zs) + [0]:
+        for d in list(range(GROUP)) if dz else far_first(GROUP):
+            pltpu.make_async_remote_copy(
+                src_ref=msg.at[rows_sent[d]], dst_ref=zbuf.at[z * GROUP + p],
+                send_sem=s1.at[0], recv_sem=r1.at[z],
+                device_id=(y * GROUP + rows_sent[d], lax.rem(z + dz, zs)), device_id_type=MESH,
+            ).start()
 
     stores = []
     for q in range(4):
@@ -160,47 +157,25 @@
     store = pltpu.make_async_copy(nbuf, newm.at[0], out_sem.at[0])
     store.start()
 
-    for copy in first:
-        copy.wait_recv()
-
-    got = lists[...].reshape(GROUP, 128)
-    top, bottom = got[0:4], got[4:8]
-    zbuf[z] = jnp.concatenate(
-        [
-            jnp.where(lane4 < 64, top, pltpu.roll(bottom, 64, 1)),
-            jnp.where(lane4 < 64, pltpu.roll(top, 64, 1), bottom),
-        ],
-        axis=0,
-    )
-    second = []
-    for d in far_first(zs):
-        copy = pltpu.make_async_remote_copy(
-            src_ref=zbuf.at[z], dst_ref=zbuf.at[z],
-            send_sem=s2.at[d - 1], recv_sem=r2.at[d - 1],
-            device_id=z_peer(d), device_id_type=MESH,
-        )
-        copy.start()
-        second.append(copy)
-    loads[4].wait()
-    loads[5].wait()
-    for copy in second:
-        copy.wait_recv()
-
-    def decode(step, total):
-        tile = zbuf[step]
-        vals = tile[0:4]
-        spot = tile[4:8].astype(jnp.int32)
+    total = jnp.zeros((SPAN, 128), F32)
+    for step in list(range(zs // 2)) + list(range(zs - 1, zs // 2 - 1, -1)):
+        slot = zbuf.at[step * GROUP : step * GROUP + GROUP]
+        pltpu.make_async_copy(slot, slot, r1.at[step]).wait()
+        tile = slot[...].reshape(GROUP, 128)
+        top, bottom = tile[0:4], tile[4:8]
+        vals = jnp.where(lane4 < 64, top, pltpu.roll(bottom, 64, 1))
+        spot = jnp.where(lane4 < 64, pltpu.roll(top, 64, 1), bottom).astype(jnp.int32)
         at_k = spot >> 6
         at_l = (spot & 63) + ((lane4 // 32) % 2) * 64
         hot_rows, hot_cols = [], []
         for c in range(4):
             hot_rows.append((row64 == at_k[c : c + 1]).astype(F32).astype(BF16))
             hot_cols.append(jnp.where(row128 == at_l[c : c + 1], vals[c : c + 1], 0.0).astype(BF16))
-        return total + mm_nt(
+        total = total + mm_nt(
             jnp.concatenate(hot_rows, axis=1), jnp.concatenate(hot_cols, axis=1)
         )
-
-    total = lax.fori_loop(0, zs, decode, jnp.zeros((SPAN, 128), F32))
+    loads[4].wait()
+    loads[5].wait()
 
     ybuf[y] = total.astype(BF16)
     third = []
@@ -238,7 +213,9 @@
         )
         copy.start()
         fourth.append(copy)
-    for copy in first + second + third:
+    sent = zbuf.at[0 : zs * GROUP - 1]
+    pltpu.make_async_copy(sent, sent, s1.at[0]).wait()
+    for copy in third:
         copy.wait_send()
     store.wait()
     for copy in fourth:
@@ -276,16 +253,13 @@
                 pltpu.VMEM((64, 192), BF16),
                 pltpu.VMEM((128, 512), F32),
                 pltpu.VMEM((GROUP, 1, 128), F32),
-                pltpu.VMEM((GROUP, 1, 128), F32),
-                pltpu.VMEM((zs, 8, 128), F32),
+                pltpu.VMEM((zs * GROUP, 1, 128), F32),
                 pltpu.VMEM((ys, SPAN, 128), BF16),
                 pltpu.VMEM((GROUP, SPAN, 128), BF16),
                 dma((6,)),
                 dma((1,)),
-                dma((GROUP - 1,)),
-                dma((GROUP - 1,)),
-                dma((max(zs - 1, 1),)),
-                dma((max(zs - 1, 1),)),
+                dma((1,)),
+                dma((zs,)),
                 dma((max(ys - 1, 1),)),
                 dma((max(ys - 1, 1),)),
                 dma((GROUP - 1,)),

time: 52.4 us -> 50.6 us (0.966)
  Pallas kernels: 49.2 us -> 47.3 us
    pallas_call x1, Pallas kernels: 49.2 us -> 47.3 us  [step(): pl.pallas_call(functools.partial(kernel, ys, zs), out_shape=(jax.ShapeDty...]
where the time goes in v2:
time: 50.6 us; the launch traced here: 50.4 us
  Pallas kernels  47.3 us (93%)
  local copies, waits for them, and re-layouts  2.42 us (5%)
  between operations  0.65 us (1%)
    pallas_call x1, Pallas kernels, step(): pl.pallas_call(functools.partial(kernel, ys, zs), out_shape=(jax.ShapeDty...  47.3 us
    unnamed x4, local copies, waits for them, and re-layouts  2.42 us

profile of v2, /device:TPU:1, one launch (start us, length us, event | category | flops | bytes accessed | tf_op | source)
XLA Modules:
  0.0 50.4 jit_solution(14571021046726268274)
XLA Ops:
  0.6 47.3 %shard_map.77 = (f32[1,128,512]{2,1,0:T(8,128)}, f32[128,512]{1,0:T(8,128)}) custom-call(f32[1,128,512]{2,1,0:T(8,128)} %mom.1, bf16[1,128,512]{2,1,0:T(8,128)(2,1)} %grad.1, s32[1,16,32]{2,1,0:T(8,128)} %idx.1, bf16[128,64]{1,0:T(8,128)(2,1)} %constant.6.clone.picker_h, bf16[256,128]{1,0:T(8,128)(2,1)} %constant.7.clone.right_h, ...), custom_call_target="tpu_custom_call" | custom-call | tf_op jit(solution)/shard_map/pallas_call | solution.py:239
  48.0 0.0 copy-start
  48.0 1.7 %copy.10 = f32[1,128,512]{2,1,0:T(8,128)} copy(f32[1,128,512]{2,1,0:T(8,128)} %get-tuple-element.4) | data formatting | bytes 524288
  49.7 0.0 copy-done
  49.7 0.7 %copy.11 = f32[128,512]{1,0:T(8,128)} copy(f32[128,512]{1,0:T(8,128)S(1)} %copy-done) | data formatting | bytes 524288
Async XLA Ops:
  48.0 1.7 %copy-start = (f32[128,512]{1,0:T(8,128)S(1)}, f32[128,512]{1,0:T(8,128)}, u32[]{:S(2)}) copy-start(f32[128,512]{1,0:T(8,128)} %get-tuple-element.5) | copy-start | bytes 786436

commit v3 on v1

--- a/solution.py
+++ b/solution.py
@@ -53,8 +53,8 @@
     ys, zs, mom, grad, idx, picker_h, right_h, left_h,
     newm, upd,
     mbuf, gbuf, ibuf, picker, right, left, nbuf,
-    msg, lists, zbuf, ybuf, ubuf,
-    in_sem, out_sem, s1, r1, s2, r2, s3, r3, s4, r4,
+    msg, lists, zown, zbuf, ybuf, ubuf,
+    in_sem, out_sem, s1, r1, s2, r2, s3, r3, s4, r4, ready,
 ):
     node = lax.axis_index("node")
     z = lax.axis_index("chip")
@@ -81,13 +81,15 @@
         return (node, lax.rem(z + d, zs))
 
     barrier = pltpu.get_barrier_semaphore()
-    peers = (
-        [z_peer(d) for d in far_first(zs)]
-        + [y_peer(d) for d in far_first(ys)]
-        + [group_peer(d) for d in far_first(GROUP)]
-    )
-    for peer in peers:
+    near = [group_peer(d) for d in far_first(GROUP)] + [y_peer(d) for d in far_first(ys)]
+    for peer in near:
         pl.semaphore_signal(barrier, inc=1, device_id=peer, device_id_type=MESH)
+
+    for dz in far_first(zs):
+
+        @pl.when(z + dz < zs)
+        def _():
+            pl.semaphore_signal(barrier, inc=1, device_id=(node, z + dz), device_id_type=MESH)
 
     lane4 = lax.broadcasted_iota(jnp.int32, (4, 128), 1)
     lane64 = lax.broadcasted_iota(jnp.int32, (SPAN, 128), 1)
@@ -137,7 +139,7 @@
         msg[2 * q + 1] = odd[q : q + 1]
     lists[p] = msg[p]
 
-    pl.semaphore_wait(barrier, len(peers))
+    pl.semaphore_wait(barrier, z + len(near))
 
     first = []
     for d in far_first(GROUP):
@@ -150,57 +152,74 @@
         copy.start()
         first.append(copy)
 
+    for dz in far_first(zs):
+
+        @pl.when(z + dz >= zs)
+        def _():
+            pl.semaphore_signal(
+                ready.at[z], inc=1, device_id=(node, z + dz - zs), device_id_type=MESH
+            )
+
     stores = []
     for q in range(4):
         rows = slice((q // 2) * 64, (q // 2) * 64 + 64)
         cols = slice((q % 2) * 256, (q % 2) * 256 + 256)
         high, low = split(rows_all[q] * picked[q])
         own = mm_nt(high, cols_high[q]) + mm_nt(low, cols_high[q]) + mm_nt(high, cols_low[q])
-        nbuf[rows, cols] = mbuf[rows, cols] - own
-    store = pltpu.make_async_copy(nbuf, newm.at[0], out_sem.at[0])
-    store.start()
+        newm[0, rows, cols] = mbuf[rows, cols] - own
 
     for copy in first:
         copy.wait_recv()
 
     got = lists[...].reshape(GROUP, 128)
     top, bottom = got[0:4], got[4:8]
-    zbuf[z] = jnp.concatenate(
+    zown[...] = jnp.concatenate(
         [
             jnp.where(lane4 < 64, top, pltpu.roll(bottom, 64, 1)),
             jnp.where(lane4 < 64, pltpu.roll(top, 64, 1), bottom),
         ],
         axis=0,
     )
-    second = []
-    for d in far_first(zs):
-        copy = pltpu.make_async_remote_copy(
-            src_ref=zbuf.at[z], dst_ref=zbuf.at[z],
-            send_sem=s2.at[d - 1], recv_sem=r2.at[d - 1],
-            device_id=z_peer(d), device_id_type=MESH,
-        )
-        copy.start()
-        second.append(copy)
+    pltpu.make_async_copy(zown, zbuf.at[z], r2.at[z]).start()
+
+    def send(to_z):
+        pltpu.make_async_remote_copy(
+            src_ref=zown, dst_ref=zbuf.at[z],
+            send_sem=s2.at[0], recv_sem=r2.at[z],
+            device_id=(node, to_z), device_id_type=MESH,
+        ).start()
+
+    for dz in far_first(zs):
+
+        @pl.when(z + dz >= zs)
+        def _():
+            send(z + dz - zs)
+
+    for dz in far_first(zs):
+
+        @pl.when(z + dz < zs)
+        def _():
+            pl.semaphore_wait(ready.at[z + dz], 1)
+            send(z + dz)
+
     loads[4].wait()
     loads[5].wait()
-    for copy in second:
-        copy.wait_recv()
-
-    def decode(step, total):
-        tile = zbuf[step]
-        vals = tile[0:4]
-        spot = tile[4:8].astype(jnp.int32)
+
+    total = jnp.zeros((SPAN, 128), F32)
+    for step in list(range(zs // 2)) + list(range(zs - 1, zs // 2 - 1, -1)):
+        slot = zbuf.at[step]
+        pltpu.make_async_copy(slot, slot, r2.at[step]).wait()
+        vals = zbuf[step, 0:4]
+        spot = zbuf[step, 4:8].astype(jnp.int32)
         at_k = spot >> 6
         at_l = (spot & 63) + ((lane4 // 32) % 2) * 64
         hot_rows, hot_cols = [], []
         for c in range(4):
             hot_rows.append((row64 == at_k[c : c + 1]).astype(F32).astype(BF16))
             hot_cols.append(jnp.where(row128 == at_l[c : c + 1], vals[c : c + 1], 0.0).astype(BF16))
-        return total + mm_nt(
+        total = total + mm_nt(
             jnp.concatenate(hot_rows, axis=1), jnp.concatenate(hot_cols, axis=1)
         )
-
-    total = lax.fori_loop(0, zs, decode, jnp.zeros((SPAN, 128), F32))
 
     ybuf[y] = total.astype(BF16)
     third = []
@@ -238,9 +257,10 @@
         )
         copy.start()
         fourth.append(copy)
-    for copy in first + second + third:
+    sent = zbuf.at[0 : zs - 1]
+    pltpu.make_async_copy(sent, sent, s2.at[0]).wait()
+    for copy in first + third:
         copy.wait_send()
-    store.wait()
     for copy in fourth:
         copy.wait_recv()
     for i in range(GROUP):
@@ -262,11 +282,11 @@
         return pl.pallas_call(
             functools.partial(kernel, ys, zs),
             out_shape=(
-                jax.ShapeDtypeStruct(momentum.shape, F32),
-                jax.ShapeDtypeStruct(momentum.shape[1:], F32),
+                pltpu.VMEM(momentum.shape, F32),
+                pltpu.VMEM(momentum.shape[1:], F32),
             ),
             in_specs=[anywhere] * 6,
-            out_specs=(anywhere, pl.BlockSpec(memory_space=pltpu.VMEM)),
+            out_specs=(pl.BlockSpec(memory_space=pltpu.VMEM), pl.BlockSpec(memory_space=pltpu.VMEM)),
             scratch_shapes=[
                 pltpu.VMEM((128, 512), F32),
                 pltpu.VMEM((128, 512), BF16),
@@ -277,6 +297,7 @@
                 pltpu.VMEM((128, 512), F32),
                 pltpu.VMEM((GROUP, 1, 128), F32),
                 pltpu.VMEM((GROUP, 1, 128), F32),
+                pltpu.VMEM((8, 128), F32),
                 pltpu.VMEM((zs, 8, 128), F32),
                 pltpu.VMEM((ys, SPAN, 128), BF16),
                 pltpu.VMEM((GROUP, SPAN, 128), BF16),
@@ -284,12 +305,13 @@
                 dma((1,)),
                 dma((GROUP - 1,)),
                 dma((GROUP - 1,)),
-                dma((max(zs - 1, 1),)),
-                dma((max(zs - 1, 1),)),
+                dma((1,)),
+                dma((zs,)),
                 dma((max(ys - 1, 1),)),
                 dma((max(ys - 1, 1),)),
                 dma((GROUP - 1,)),
                 dma((GROUP - 1,)),
+                pltpu.SemaphoreType.REGULAR((zs,)),
             ],
             compiler_params=pltpu.CompilerParams(collective_id=0, has_side_effects=True),
         )(momentum, gradient, indices, *(jnp.asarray(t) for t in tables))

time: 52.4 us -> 43.5 us (0.83)
  Pallas kernels: 49.2 us -> 41.3 us
  local copies, waits for them, and re-layouts: 2.42 us -> 1.41 us
    pallas_call x1, Pallas kernels: 49.2 us -> 41.3 us  [step(): pl.pallas_call(functools.partial(kernel, ys, zs), out_shape=(pltpu.VMEM(m...]
    unnamed x4 -> x2, local copies, waits for them, and re-layouts: 2.42 us -> 1.41 us
where the time goes in v3:
time: 43.5 us; the launch traced here: 43.4 us
  Pallas kernels  41.3 us (95%)
  local copies, waits for them, and re-layouts  1.41 us (3%)
  between operations  0.64 us (1%)
    pallas_call x1, Pallas kernels, step(): pl.pallas_call(functools.partial(kernel, ys, zs), out_shape=(pltpu.VMEM(m...  41.3 us
    unnamed x2, local copies, waits for them, and re-layouts  1.41 us

profile of v3, /device:TPU:1, one launch (start us, length us, event | category | flops | bytes accessed | tf_op | source)
XLA Modules:
  0.0 43.4 jit_solution(7631027784979125632)
XLA Ops:
  0.6 41.3 %shard_map.77 = (f32[1,128,512]{2,1,0:T(8,128)S(1)}, f32[128,512]{1,0:T(8,128)S(1)}) custom-call(f32[1,128,512]{2,1,0:T(8,128)} %mom.1, bf16[1,128,512]{2,1,0:T(8,128)(2,1)} %grad.1, s32[1,16,32]{2,1,0:T(8,128)} %idx.1, bf16[128,64]{1,0:T(8,128)(2,1)} %constant.6.clone.picker_h, bf16[256,128]{1,0:T(8,128)(2,1)} %constant.7.clone.right_h, ...), custom_call_target="tpu_custom_call" | custom-call | tf_op jit(solution)/shard_map/pallas_call | solution.py:282
  42.0 0.7 %copy.10 = f32[1,128,512]{2,1,0:T(8,128)} copy(f32[1,128,512]{2,1,0:T(8,128)S(1)} %get-tuple-element.2) | data formatting | bytes 524288
  42.7 0.7 %copy.11 = f32[128,512]{1,0:T(8,128)} copy(f32[128,512]{1,0:T(8,128)S(1)} %get-tuple-element.3) | data formatting | bytes 524288
